TPU v7x, 32 devices: a whole 2x2x4 slice. The times are simulated.
32 devices in a mesh: groups: 2 (over y), tx: 4 (over z), ty: 2 (over x), ka: 2 (over core).
Axes of the slice: x: 2, y: 2, z: 4, core: 2. Of those that a mesh axis runs over, the one named last changes fastest.
Arguments:
- mask_raster: float32 [2048, 512], P(('groups', 'tx'), 'ty'), parts along dimension 0, may hold values from 0 to 1
- frag_rows: int32 [8, 2, 512], P(('groups', 'tx'), 'ty'), parts along dimension 0, may hold values from 8 to 215
- frag_cols: int32 [8, 2, 512], P(('groups', 'tx'), 'ty'), parts along dimension 0, may hold values from 8 to 215
- frag_length: int32 [8, 2, 512], P(('groups', 'tx'), 'ty'), parts along dimension 0, may hold values from 4 to 32
- frag_orient: int32 [8, 2, 512], P(('groups', 'tx'), 'ty'), parts along dimension 0, may hold values from 0 to 1
- frag_moves: int32 [8, 2, 2, 512], P(('groups', 'tx'), 'ty'), parts along dimension 0, may hold values from -4 to 4
- site_rows: int32 [8, 2, 2048], P(('groups', 'tx'), 'ty'), parts along dimension 0, may hold values from 1 to 254
- site_cols: int32 [8, 2, 2048], P(('groups', 'tx'), 'ty'), parts along dimension 0, may hold values from 1 to 254
- spectra: float32 [16, 2, 128, 128], P('ka'), may hold values from -24 to 24
- weights: float32 [16], P('ka'), may hold values from 0.05 to 1
- tolerance: int32 [2], replicated, may hold values from 1 to 16
Outputs:
- intensity: float32 [2048, 512], P(('groups', 'tx'), 'ty'), parts along dimension 0
- corrected_mask: float32 [2048, 512], P(('groups', 'tx'), 'ty'), parts along dimension 0
- edge_errors: float32 [8, 2, 2, 2048], P(('groups', 'tx'), 'ty'), parts along dimension 0
- peak_error: float32 [4], P('groups'), parts along dimension 0
- converged_share: float32 [4], P('groups'), parts along dimension 0
There are 2 independent parts, one for each index of `groups`. A program takes and returns all parts, laid end to end along the dimension named above; an argument that names none is the same for every part. Nothing has to cross between parts.
All inputs are finite; a program needn't handle non-finite values.
Results may differ from a plain program's by a relative error of at most 0.0003.
Values sent between devices are 32-bit elements; how exact they have to be, the bound alone decides.
A program may use at most 64 MiB of HBM per device.

v0:
```python
import functools
import math

import jax
import jax.numpy as jnp
import ml_dtypes
import numpy as np
from jax import lax
from jax.experimental import pallas as pl
from jax.experimental.pallas import tpu as pltpu
from jax.sharding import PartitionSpec as P

HALO = 128
BAND = 128
ITERS = 2

LEVEL = 0.4
SLOPE_FLOOR = 0.05
SHARPNESS = 8.0
CHUNK = 256
OPERANDS = 18
MESH = pl.DeviceIdType.MESH
F32 = jnp.float32
BF16 = jnp.bfloat16


def pieces_of(table):
    high = table.astype(ml_dtypes.bfloat16)
    rest = table - high.astype(np.float64)
    middle = rest.astype(ml_dtypes.bfloat16)
    low = (rest - middle.astype(np.float64)).astype(ml_dtypes.bfloat16)
    return high, middle, low


def tables(tile):
    ext = tile + 2 * HALO
    half = BAND // 2
    step = 2.0 * math.pi / ext
    rows = -(-(2 * half + 1) // 16) * 16
    span = np.arange(ext) - (ext - 1) / 2
    positive = np.arange(half + 1)
    freq = np.arange(BAND) - half
    forward = np.zeros((rows, ext))
    forward[: half + 1] = np.cos(step * positive[:, None] * span[None])
    forward[half + 1 : 2 * half + 1] = np.sin(step * positive[1:, None] * span[None])
    phase = step * span[:, None] * freq[None]
    across = np.concatenate([np.cos(phase), np.sin(phase)], axis=1)
    expand = np.zeros((2 * BAND, 2 * BAND))
    for place, number in enumerate(freq):
        expand[place, abs(number)] = 1.0
        if number != 0:
            expand[BAND + place, half + abs(number)] = np.sign(number)
    angle = step * (np.arange(tile // 2)[:, None] + 0.5) * freq[None]
    back_rows = np.concatenate([np.cos(angle), np.sin(angle)], axis=0) / ext
    back_cols = np.concatenate([np.cos(angle.T), np.sin(angle.T)], axis=1) / ext
    flip = np.eye(tile // 2)[::-1].astype(ml_dtypes.bfloat16)
    high, middle, low = pieces_of(back_rows)
    rows6 = np.concatenate([high, high, middle, high, middle, low], axis=1)
    high, middle, low = pieces_of(back_cols)
    cols6 = np.concatenate([high, high, middle, high, middle, low], axis=0)
    return (
        np.concatenate(pieces_of(forward), axis=0),
        np.concatenate(pieces_of(across), axis=0),
        np.concatenate([expand] * 3, axis=1).astype(ml_dtypes.bfloat16),
        rows6,
        cols6,
        np.concatenate([flip] * 3, axis=1),
        np.concatenate([flip] * 3, axis=0),
    )


def split(value):
    high = value.astype(BF16)
    low = (value - high.astype(F32)).astype(BF16)
    return high, low


def split3(value):
    high = value.astype(BF16)
    rest = value - high.astype(F32)
    middle = rest.astype(BF16)
    low = (rest - middle.astype(F32)).astype(BF16)
    return high, middle, low


def dot(left, right):
    return jnp.dot(left, right, preferred_element_type=F32)


def strip_sum(row_start, col_start, frag_len, orient, shift, extent):
    lower = jnp.minimum(shift, 0)
    upper = jnp.maximum(shift, 0)
    along = orient == 0
    row_low = jnp.where(along, row_start, row_start + lower)
    row_high = jnp.where(along, row_start + frag_len, row_start + upper)
    col_low = jnp.where(along, col_start + lower, col_start)
    col_high = jnp.where(along, col_start + upper, col_start + frag_len)
    position = lax.broadcasted_iota(jnp.int32, (extent, shift.shape[1]), 0)
    signs = jnp.where(shift > 0, 1.0, jnp.where(shift < 0, -1.0, 0.0))
    row_select = jnp.where((position >= row_low) & (position < row_high), signs, 0.0).astype(BF16)
    col_select = jnp.where((position >= col_low) & (position < col_high), 1.0, 0.0).astype(BF16)
    return lax.dot_general(
        row_select, col_select, (((1,), (1,)), ((), ())), preferred_element_type=F32
    )


def kernel(sizes, *refs):
    away, outs = refs[:OPERANDS], refs[OPERANDS : OPERANDS + 5]
    here, rest = refs[OPERANDS + 5 : 2 * OPERANDS + 5], refs[2 * OPERANDS + 5 :]
    sems = rest[-1]
    copies = [
        pltpu.make_async_copy(src, dst, sems.at[i]) for i, (src, dst) in enumerate(zip(away, here))
    ]

    def need(*numbers):
        for number in numbers:
            copies[number].wait()

    def start(*numbers):
        for number in numbers:
            copies[number].start()

    body(sizes, start, need, away[8], *here, *outs, *rest[:-1])


def body(
    sizes,
    begin,
    need,
    spec_away,
    mask_ref,
    frow_ref,
    fcol_ref,
    flen_ref,
    fori_ref,
    fmove_ref,
    srow_ref,
    scol_ref,
    spec_ref,
    weight_ref,
    tol_ref,
    forward_ref,
    across_ref,
    expand_ref,
    rows_ref,
    cols_ref,
    flip_wide_ref,
    flip_tall_ref,
    intensity_ref,
    mask_out_ref,
    errors_ref,
    peaks_ref,
    shares_ref,
    ext,
    hext,
    spec_rx,
    wv,
    wv_rx,
    sbuf,
    folded,
    img,
    img_rx,
    err,
    err_rx,
    stat,
    stat_rx,
    halo_send,
    halo_recv,
    ka_send,
    ka_recv,
    stat_send,
    stat_recv,
):
    n_tx, n_ty, n_ka = sizes
    count = n_tx * n_ty * n_ka
    tile = mask_ref.shape[0]
    wide = ext.shape[0]
    sites = srow_ref.shape[2]
    kernels = spec_ref.shape[0]
    group = lax.axis_index("groups")
    tx = lax.axis_index("tx")
    ty = lax.axis_index("ty")
    ka = lax.axis_index("ka")
    me = (tx * n_ty + ty) * n_ka + ka

    def place(number):
        return (
            group,
            lax.div(number, n_ty * n_ka),
            lax.rem(lax.div(number, n_ka), n_ty),
            lax.rem(number, n_ka),
        )

    def remote(src, dst, send, recv, target):
        return pltpu.make_async_remote_copy(
            src_ref=src, dst_ref=dst, send_sem=send, recv_sem=recv, device_id=target, device_id_type=MESH
        )

    begin(1, 2, 3, 4, 5, 0, 9, 11, 12, 8, 13, 14, 15, 16, 17, 6, 7, 10)
    barrier = pltpu.get_barrier_semaphore()

    def greet(offset, carry):
        pl.semaphore_signal(
            barrier, inc=1, device_id=place(lax.rem(me + offset, count)), device_id_type=MESH
        )
        return carry

    lax.fori_loop(1, count, greet, 0)

    need(1, 2, 3, 4, 5, 0)
    fragments = (frow_ref[0], fcol_ref[0], flen_ref[0], fori_ref[0])
    first = jnp.clip(mask_ref[...] + strip_sum(*fragments, fmove_ref[0, 0, 0:1, :], tile), 0.0, 1.0)
    second = jnp.clip(first + strip_sum(*fragments, fmove_ref[0, 0, 1:2, :], tile), 0.0, 1.0)
    mask_out_ref[...] = second
    ext[HALO : HALO + tile, :] = jnp.where(ka == 0, first, second)
    need(9)
    for k in range(kernels):
        wv[k : k + 1, :] = jnp.full((1, 128), weight_ref[k], F32)

    pl.semaphore_wait(barrier, count - 1)

    partner = (group, tx, ty, 1 - ka)
    up = (group, tx - 1, ty, ka)
    down = (group, tx + 1, ty, ka)
    left = (group, tx, ty - 1, ka)
    right = (group, tx, ty + 1, ka)
    to_up = remote(
        ext.at[pl.ds(HALO, HALO)], ext.at[pl.ds(HALO + tile, HALO)], halo_send.at[0], halo_recv.at[0], up
    )
    to_down = remote(
        ext.at[pl.ds(tile, HALO)], ext.at[pl.ds(0, HALO)], halo_send.at[1], halo_recv.at[1], down
    )

    @pl.when(tx > 0)
    def _():
        to_up.start()

    @pl.when(tx < n_tx - 1)
    def _():
        to_down.start()

    to_spec = remote(spec_away, spec_rx, ka_send.at[0], ka_recv.at[0], partner)
    to_wv = remote(wv, wv_rx, ka_send.at[1], ka_recv.at[1], partner)
    to_spec.start()
    to_wv.start()

    @pl.when(tx == 0)
    def _():
        ext[0:HALO, :] = jnp.zeros((HALO, tile), F32)

    @pl.when(tx == n_tx - 1)
    def _():
        ext[HALO + tile : wide, :] = jnp.zeros((HALO, tile), F32)

    @pl.when(ty == 0)
    def _():
        hext[0] = jnp.zeros(hext.shape[1:], F32)

    @pl.when(ty == n_ty - 1)
    def _():
        hext[3] = jnp.zeros(hext.shape[1:], F32)

    @pl.when(tx > 0)
    def _():
        to_down.wait_recv()

    @pl.when(tx < n_tx - 1)
    def _():
        to_up.wait_recv()

    rows = hext.shape[1]
    need(11)
    high, middle, low = split3(ext[...])
    by_high = dot(forward_ref[...], high)
    by_middle = dot(forward_ref[0 : 2 * rows, :], middle)
    by_low = dot(forward_ref[0:rows, :], low)
    half = (by_low + by_high[2 * rows :] + by_middle[rows:]) + (by_high[rows : 2 * rows] + by_middle[:rows])
    half = half + by_high[:rows]
    hext[1] = half[:, :HALO]
    hext[2] = half[:, HALO:]
    to_left = remote(hext.at[1], hext.at[3], halo_send.at[2], halo_recv.at[2], left)
    to_right = remote(hext.at[2], hext.at[0], halo_send.at[3], halo_recv.at[3], right)

    @pl.when(ty > 0)
    def _():
        to_left.start()

    @pl.when(ty < n_ty - 1)
    def _():
        to_right.start()

    @pl.when(ty > 0)
    def _():
        to_right.wait_recv()

    @pl.when(ty < n_ty - 1)
    def _():
        to_left.wait_recv()

    need(12, 13)
    whole = jnp.concatenate([hext[0], hext[1], hext[2], hext[3]], axis=1)
    high, middle, low = split3(whole)
    by_high = dot(jnp.concatenate([high, middle, low], axis=0), across_ref[0:wide, :])
    by_middle = dot(jnp.concatenate([high, middle], axis=0), across_ref[wide : 2 * wide, :])
    by_low = dot(high, across_ref[2 * wide :, :])
    full = (by_low + by_high[2 * rows :] + by_middle[rows:]) + (by_high[rows : 2 * rows] + by_middle[:rows])
    full = full + by_high[:rows]
    full = jnp.concatenate([full, jnp.zeros((2 * BAND - rows, 2 * BAND), F32)], axis=0)
    mixed = dot(expand_ref[...], jnp.concatenate(split3(full), axis=0))
    sbuf[0] = mixed[:BAND, :BAND] - mixed[BAND:, BAND:]
    sbuf[1] = -(mixed[BAND:, :BAND] + mixed[:BAND, BAND:])

    mid = tile // 2
    folded[...] = jnp.zeros_like(folded)

    def kernel_image(spectra, scales, k):
        scale = jnp.sqrt(scales[pl.ds(k, 1), :])
        k_re = spectra[k, 0] * scale
        k_im = spectra[k, 1] * scale
        s_re = sbuf[0]
        s_im = sbuf[1]
        p_re = k_re * s_re - k_im * s_im
        p_im = k_re * s_im + k_im * s_re
        high, middle, low = split3(jnp.concatenate([p_re, p_im], axis=1))
        parts = dot(
            rows_ref[...], jnp.concatenate([high, middle, high, low, middle, high], axis=0)
        )
        even_re, even_im = parts[:mid, :BAND], parts[:mid, BAND:]
        odd_re, odd_im = parts[mid:, :BAND], parts[mid:, BAND:]
        inner = jnp.concatenate(
            [even_re - odd_im, even_re + odd_im, even_im + odd_re, even_im - odd_re], axis=0
        )
        high, middle, low = split3(inner)
        turned = dot(
            jnp.concatenate([high, middle, high, low, middle, high], axis=1), cols_ref[...]
        )
        re_cos, re_sin = turned[:tile, :mid], turned[:tile, mid:]
        im_cos, im_sin = turned[tile:, :mid], turned[tile:, mid:]
        f_re, f_im = re_cos - im_sin, im_cos + re_sin
        near = f_re * f_re + f_im * f_im
        f_re, f_im = re_cos + im_sin, im_cos - re_sin
        return near, f_re * f_re + f_im * f_im

    def add_pair(spectra, scales, k):
        near_a, far_a = kernel_image(spectra, scales, 4 * k)
        near_b, far_b = kernel_image(spectra, scales, 4 * k + 1)
        near_c, far_c = kernel_image(spectra, scales, 4 * k + 2)
        near_d, far_d = kernel_image(spectra, scales, 4 * k + 3)
        folded[:, :mid] += (near_a + near_b) + (near_c + near_d)
        folded[:, mid:] += (far_a + far_b) + (far_c + far_d)

    def add_one(spectra, scales, k):
        near, far = kernel_image(spectra, scales, k)
        folded[:, :mid] += near
        folded[:, mid:] += far

    def own_step(k, carry):
        add_pair(spec_ref, wv, k)
        return carry

    def rx_step(k, carry):
        add_pair(spec_rx, wv_rx, k)
        return carry

    need(8, 14, 15)
    lax.fori_loop(0, kernels // 4, own_step, 0)
    for k in range(kernels // 4 * 4, kernels):
        add_one(spec_ref, wv, k)
    to_spec.wait_recv()
    to_wv.wait_recv()
    lax.fori_loop(0, kernels // 4, rx_step, 0)
    for k in range(kernels // 4 * 4, kernels):
        add_one(spec_rx, wv_rx, k)

    need(16, 17)
    lower = jnp.concatenate(split3(folded[mid:, :]), axis=0)
    ordered = jnp.concatenate([dot(flip_wide_ref[...], lower), folded[:mid, :]], axis=0)
    lower = jnp.concatenate(split3(ordered[:, mid:]), axis=1)
    img[...] = jnp.concatenate([dot(lower, flip_tall_ref[...]), ordered[:, :mid]], axis=1)
    to_img = remote(img, img_rx, ka_send.at[2], ka_recv.at[2], partner)
    to_img.start()

    image = img[...]
    grad_rows = (pltpu.roll(image, tile - 1, 0) - pltpu.roll(image, 1, 0)) * 0.5
    grad_cols = (pltpu.roll(image, tile - 1, 1) - pltpu.roll(image, 1, 1)) * 0.5
    slope = jnp.sqrt(grad_rows * grad_rows + grad_cols * grad_cols)
    error_map = (image - LEVEL) / jnp.maximum(slope, SLOPE_FLOOR)
    high, low = split(error_map)
    maps = jnp.concatenate([high, low], axis=1)
    position = lax.broadcasted_iota(jnp.int32, (tile, CHUNK), 0)
    need(6, 7, 10)
    limit = tol_ref[ka].astype(F32) / 8.0
    peak = jnp.zeros((1, CHUNK), F32)
    total = jnp.zeros((1, CHUNK), F32)
    for start in range(0, sites, CHUNK):
        at_rows = srow_ref[0, :, start : start + CHUNK]
        at_cols = scol_ref[0, :, start : start + CHUNK]
        choose = jnp.where(position == at_cols, 1.0, 0.0).astype(BF16)
        picked = dot(maps, jnp.concatenate([choose, choose], axis=0))
        errors = jnp.sum(jnp.where(position == at_rows, picked, 0.0), axis=0, keepdims=True)
        err[:, start : start + CHUNK] = errors
        size = jnp.abs(errors)
        peak = jnp.maximum(peak, size)
        total = total + 1.0 / (1.0 + jnp.exp(-SHARPNESS * (limit - size)))
    stat[0:1, :] = jnp.full((1, 128), jnp.max(peak), F32)
    stat[1:2, :] = jnp.full((1, 128), jnp.sum(total), F32)
    to_err = remote(err, err_rx, ka_send.at[3], ka_recv.at[3], partner)
    to_err.start()

    def to_stat(offset):
        return remote(
            stat,
            stat_rx.at[offset],
            stat_send.at[offset],
            stat_recv.at[offset],
            place(lax.rem(me + offset, count)),
        )

    def send_stat(offset, carry):
        to_stat(offset).start()
        return carry

    lax.fori_loop(1, count, send_stat, 0)

    to_img.wait_recv()
    intensity_ref[...] = jnp.where(ka == ITERS - 1, image, img_rx[...])
    to_err.wait_recv()
    mine = err[...]
    theirs = err_rx[...]
    errors_ref[0, 0, 0:1, :] = jnp.where(ka == 0, mine, theirs)
    errors_ref[0, 0, 1:2, :] = jnp.where(ka == 0, theirs, mine)

    def wait_stat(offset, carry):
        to_stat(offset).wait()
        return carry

    lax.fori_loop(1, count, wait_stat, 0)

    mine_peak, mine_total = stat[0:1, :], stat[1:2, :]
    their_peak = jnp.zeros((1, 128), F32)
    their_total = jnp.zeros((1, 128), F32)
    for offset in range(1, count):
        peak_in, total_in = stat_rx[offset, 0:1, :], stat_rx[offset, 1:2, :]
        if offset % n_ka == 0:
            mine_peak = jnp.maximum(mine_peak, peak_in)
            mine_total = mine_total + total_in
        else:
            their_peak = jnp.maximum(their_peak, peak_in)
            their_total = their_total + total_in
    scale = 1.0 / (sites * n_tx * n_ty)
    peak_a, peak_b = jnp.max(mine_peak), jnp.max(their_peak)
    share_a, share_b = jnp.max(mine_total) * scale, jnp.max(their_total) * scale
    peaks_ref[0] = jnp.where(ka == 0, peak_a, peak_b)
    peaks_ref[1] = jnp.where(ka == 0, peak_b, peak_a)
    shares_ref[0] = jnp.where(ka == 0, share_a, share_b)
    shares_ref[1] = jnp.where(ka == 0, share_b, share_a)

    @pl.when(tx > 0)
    def _():
        to_up.wait_send()

    @pl.when(tx < n_tx - 1)
    def _():
        to_down.wait_send()

    @pl.when(ty > 0)
    def _():
        to_left.wait_send()

    @pl.when(ty < n_ty - 1)
    def _():
        to_right.wait_send()

    for copy in (to_spec, to_wv, to_img, to_err):
        copy.wait_send()


def shards(sizes, *args):
    mask_raster, spectra = args[0], args[8]
    site_count = args[6].shape[2]
    tile = mask_raster.shape[0]
    wide = tile + 2 * HALO
    consts = [jnp.asarray(a) for a in tables(tile)]
    rows = consts[0].shape[0] // 3
    kernels = spectra.shape[0]
    count = sizes[0] * sizes[1] * sizes[2]
    vmem = pl.BlockSpec(memory_space=pltpu.VMEM)
    smem = pl.BlockSpec(memory_space=pltpu.SMEM)
    dma = pltpu.SemaphoreType.DMA
    operands = (*args, *consts)
    local = [
        (pltpu.SMEM if number in (9, 10) else pltpu.VMEM)(a.shape, a.dtype)
        for number, a in enumerate(operands)
    ]
    return tuple(
        pl.pallas_call(
            functools.partial(kernel, sizes),
            out_shape=(
                jax.ShapeDtypeStruct((tile, tile), F32),
                jax.ShapeDtypeStruct((tile, tile), F32),
                jax.ShapeDtypeStruct((1, 1, ITERS, site_count), F32),
                jax.ShapeDtypeStruct((ITERS,), F32),
                jax.ShapeDtypeStruct((ITERS,), F32),
            ),
            in_specs=[pl.BlockSpec(memory_space=pltpu.HBM)] * OPERANDS,
            out_specs=(vmem, vmem, vmem, smem, smem),
            scratch_shapes=local
            + [
                pltpu.VMEM((wide, tile), F32),
                pltpu.VMEM((4, rows, HALO), F32),
                pltpu.VMEM(spectra.shape, F32),
                pltpu.VMEM((kernels, 128), F32),
                pltpu.VMEM((kernels, 128), F32),
                pltpu.VMEM((2, BAND, BAND), F32),
                pltpu.VMEM((tile, tile), F32),
                pltpu.VMEM((tile, tile), F32),
                pltpu.VMEM((tile, tile), F32),
                pltpu.VMEM((1, site_count), F32),
                pltpu.VMEM((1, site_count), F32),
                pltpu.VMEM((8, 128), F32),
                pltpu.VMEM((count, 8, 128), F32),
                dma((4,)),
                dma((4,)),
                dma((4,)),
                dma((4,)),
                dma((count,)),
                dma((count,)),
                dma((OPERANDS,)),
            ],
            compiler_params=pltpu.CompilerParams(
                collective_id=0, has_side_effects=True
            ),
        )(*operands)
    )


def solution(mesh):
    sizes = tuple(mesh.shape[axis] for axis in ("tx", "ty", "ka"))
    assert sizes[2] == ITERS
    placed = (
        P(("groups", "tx"), "ty"),
        P(("groups", "tx"), "ty", None),
        P(("groups", "tx"), "ty", None),
        P(("groups", "tx"), "ty", None),
        P(("groups", "tx"), "ty", None),
        P(("groups", "tx"), "ty", None, None),
        P(("groups", "tx"), "ty", None),
        P(("groups", "tx"), "ty", None),
        P("ka", None, None, None),
        P("ka"),
        P(),
    )
    return jax.shard_map(
        functools.partial(shards, sizes),
        mesh=mesh,
        in_specs=placed,
        out_specs=(
            P(("groups", "tx"), "ty"),
            P(("groups", "tx"), "ty"),
            P(("groups", "tx"), "ty", None, None),
            P("groups"),
            P("groups"),
        ),
        check_vma=False,
    )
```

profile of v0, /device:TPU:0, one launch (start us, length us, event | category | flops | bytes accessed | tf_op | source)
XLA Modules:
  0.0 34.5 jit_solution(6978788106342822208)
XLA Ops:
  0.6 29.6 %shard_map.209 = (f32[256,256]{1,0:T(8,128)}, f32[256,256]{1,0:T(8,128)}, f32[1,1,2,2048]{3,2,1,0:T(2,128)}, f32[2]{0:T(128)}, f32[2]{0:T(128)}) custom-call(f32[256,256]{1,0:T(8,128)} %refs_0_.1, s32[1,1,512]{2,1,0:T(1,128)} %refs_1_.1, s32[1,1,512]{2,1,0:T(1,128)} %refs_2_.1, s32[1,1,512]{2,1,0:T(1,128)} %refs_3_.1, s32[1,1,512]{2,1,0:T(1,128)} %refs_4_.1, ...), custom_call_target="tpu_custom_call" | custom-call | tf_op jit(solution)/shard_map/pallas_call | solution.py:496
  30.3 0.0 copy-start
  30.3 1.7 %copy.28 = f32[256,256]{1,0:T(8,128)} copy(f32[256,256]{1,0:T(8,128)} %get-tuple-element.10) | data formatting | bytes 524288
  32.0 0.0 copy-done
  32.0 0.0 copy-start.1
  32.0 0.7 %copy.29 = f32[256,256]{1,0:T(8,128)} copy(f32[256,256]{1,0:T(8,128)S(1)} %copy-done) | data formatting | bytes 524288
  32.7 0.0 copy-done.1
  32.7 0.0 copy-start.3
  32.7 0.6 %copy.30 = f32[1,1,2,2048]{3,2,1,0:T(2,128)} copy(f32[1,1,2,2048]{3,2,1,0:T(2,128)S(1)} %copy-done.1) | data formatting | bytes 32768
  33.3 0.1 copy-done.3
  33.4 0.0 copy-start.2
  33.4 0.5 %copy.31 = f32[2]{0:T(128)} copy(f32[2]{0:T(128)S(1)} %copy-done.3) | data formatting | bytes 16
  33.9 0.1 copy-done.2
  34.0 0.5 %copy.32 = f32[2]{0:T(128)} copy(f32[2]{0:T(128)S(1)} %copy-done.2) | data formatting | bytes 16
Async XLA Ops:
  30.3 1.7 %copy-start = (f32[256,256]{1,0:T(8,128)S(1)}, f32[256,256]{1,0:T(8,128)}, u32[]{:S(2)}) copy-start(f32[256,256]{1,0:T(8,128)} %get-tuple-element.11) | copy-start | bytes 786436
  32.0 0.7 %copy-start.1 = (f32[1,1,2,2048]{3,2,1,0:T(2,128)S(1)}, f32[1,1,2,2048]{3,2,1,0:T(2,128)}, u32[]{:S(2)}) copy-start(f32[1,1,2,2048]{3,2,1,0:T(2,128)} %get-tuple-element.12) | copy-start | bytes 49156
  32.7 0.7 %copy-start.3 = (f32[2]{0:T(128)S(1)}, f32[2]{0:T(128)}, u32[]{:S(2)}) copy-start(f32[2]{0:T(128)} %get-tuple-element.13) | copy-start | bytes 28
  33.4 0.6 %copy-start.2 = (f32[2]{0:T(128)S(1)}, f32[2]{0:T(128)}, u32[]{:S(2)}) copy-start(f32[2]{0:T(128)} %get-tuple-element.14) | copy-start | bytes 28
where the time goes:
time: 34.8 us; the launch traced here: 34.5 us
  Pallas kernels  29.6 us (85%)
  local copies, waits for them, and re-layouts  4.2 us (12%)
  between operations  0.66 us (2%)
    pallas_call x1, Pallas kernels, shards(): pl.pallas_call(functools.partial(kernel, sizes), out_shape=(jax.ShapeDtyp...  29.6 us
    unnamed x13, local copies, waits for them, and re-layouts  4.2 us

commit v1 on v0

--- a/solution.py
+++ b/solution.py
@@ -19,6 +19,7 @@
 SHARPNESS = 8.0
 CHUNK = 256
 OPERANDS = 18
+VMEM_LIMIT = 32 * 1024 * 1024
 MESH = pl.DeviceIdType.MESH
 F32 = jnp.float32
 BF16 = jnp.bfloat16
@@ -105,8 +106,8 @@
 
 
 def kernel(sizes, *refs):
-    away, outs = refs[:OPERANDS], refs[OPERANDS : OPERANDS + 5]
-    here, rest = refs[OPERANDS + 5 : 2 * OPERANDS + 5], refs[2 * OPERANDS + 5 :]
+    away, outs = refs[:OPERANDS], refs[OPERANDS : OPERANDS + 4]
+    here, rest = refs[OPERANDS + 4 : 2 * OPERANDS + 4], refs[2 * OPERANDS + 4 :]
     sems = rest[-1]
     copies = [
         pltpu.make_async_copy(src, dst, sems.at[i]) for i, (src, dst) in enumerate(zip(away, here))
@@ -149,8 +150,7 @@
     intensity_ref,
     mask_out_ref,
     errors_ref,
-    peaks_ref,
-    shares_ref,
+    stats_ref,
     ext,
     hext,
     spec_rx,
@@ -158,6 +158,7 @@
     wv_rx,
     sbuf,
     folded,
+    choose,
     img,
     img_rx,
     err,
@@ -244,6 +245,12 @@
     to_spec.start()
     to_wv.start()
 
+    need(7)
+    position = lax.broadcasted_iota(jnp.int32, (tile, CHUNK), 0)
+    for start in range(0, sites, CHUNK):
+        at_cols = scol_ref[0, :, start : start + CHUNK]
+        choose[:, start : start + CHUNK] = jnp.where(position == at_cols, 1.0, 0.0).astype(BF16)
+
     @pl.when(tx == 0)
     def _():
         ext[0:HALO, :] = jnp.zeros((HALO, tile), F32)
@@ -386,33 +393,33 @@
     slope = jnp.sqrt(grad_rows * grad_rows + grad_cols * grad_cols)
     error_map = (image - LEVEL) / jnp.maximum(slope, SLOPE_FLOOR)
     high, low = split(error_map)
-    maps = jnp.concatenate([high, low], axis=1)
-    position = lax.broadcasted_iota(jnp.int32, (tile, CHUNK), 0)
-    need(6, 7, 10)
+    need(6, 10)
     limit = tol_ref[ka].astype(F32) / 8.0
     peak = jnp.zeros((1, CHUNK), F32)
     total = jnp.zeros((1, CHUNK), F32)
     for start in range(0, sites, CHUNK):
         at_rows = srow_ref[0, :, start : start + CHUNK]
-        at_cols = scol_ref[0, :, start : start + CHUNK]
-        choose = jnp.where(position == at_cols, 1.0, 0.0).astype(BF16)
-        picked = dot(maps, jnp.concatenate([choose, choose], axis=0))
+        picked = dot(high, choose[:, start : start + CHUNK]) + dot(low, choose[:, start : start + CHUNK])
         errors = jnp.sum(jnp.where(position == at_rows, picked, 0.0), axis=0, keepdims=True)
         err[:, start : start + CHUNK] = errors
         size = jnp.abs(errors)
         peak = jnp.maximum(peak, size)
         total = total + 1.0 / (1.0 + jnp.exp(-SHARPNESS * (limit - size)))
-    stat[0:1, :] = jnp.full((1, 128), jnp.max(peak), F32)
-    stat[1:2, :] = jnp.full((1, 128), jnp.sum(total), F32)
+    stat[0:1, :] = functools.reduce(
+        jnp.maximum, [peak[:, i : i + 128] for i in range(0, CHUNK, 128)]
+    )
+    stat[1:2, :] = functools.reduce(
+        jnp.add, [total[:, i : i + 128] for i in range(0, CHUNK, 128)]
+    )
     to_err = remote(err, err_rx, ka_send.at[3], ka_recv.at[3], partner)
     to_err.start()
 
     def to_stat(offset):
         return remote(
             stat,
-            stat_rx.at[offset],
+            stat_rx.at[me],
             stat_send.at[offset],
-            stat_recv.at[offset],
+            stat_recv.at[me],
             place(lax.rem(me + offset, count)),
         )
 
@@ -421,6 +428,7 @@
         return carry
 
     lax.fori_loop(1, count, send_stat, 0)
+    stat_rx[pl.ds(me, 1)] = stat[...][None]
 
     to_img.wait_recv()
     intensity_ref[...] = jnp.where(ka == ITERS - 1, image, img_rx[...])
@@ -431,29 +439,23 @@
     errors_ref[0, 0, 1:2, :] = jnp.where(ka == 0, theirs, mine)
 
     def wait_stat(offset, carry):
-        to_stat(offset).wait()
+        to_stat(offset).wait_send()
+        source = lax.rem(me + offset, count)
+        remote(
+            stat, stat_rx.at[source], stat_send.at[offset], stat_recv.at[source], place(source)
+        ).wait_recv()
         return carry
 
     lax.fori_loop(1, count, wait_stat, 0)
 
-    mine_peak, mine_total = stat[0:1, :], stat[1:2, :]
-    their_peak = jnp.zeros((1, 128), F32)
-    their_total = jnp.zeros((1, 128), F32)
-    for offset in range(1, count):
-        peak_in, total_in = stat_rx[offset, 0:1, :], stat_rx[offset, 1:2, :]
-        if offset % n_ka == 0:
-            mine_peak = jnp.maximum(mine_peak, peak_in)
-            mine_total = mine_total + total_in
-        else:
-            their_peak = jnp.maximum(their_peak, peak_in)
-            their_total = their_total + total_in
-    scale = 1.0 / (sites * n_tx * n_ty)
-    peak_a, peak_b = jnp.max(mine_peak), jnp.max(their_peak)
-    share_a, share_b = jnp.max(mine_total) * scale, jnp.max(their_total) * scale
-    peaks_ref[0] = jnp.where(ka == 0, peak_a, peak_b)
-    peaks_ref[1] = jnp.where(ka == 0, peak_b, peak_a)
-    shares_ref[0] = jnp.where(ka == 0, share_a, share_b)
-    shares_ref[1] = jnp.where(ka == 0, share_b, share_a)
+    for which in range(ITERS):
+        rows_of = range(which, count, n_ka)
+        stats_ref[which : which + 1, :] = functools.reduce(
+            jnp.maximum, [stat_rx[number, 0:1, :] for number in rows_of]
+        )
+        stats_ref[ITERS + which : ITERS + which + 1, :] = functools.reduce(
+            jnp.add, [stat_rx[number, 1:2, :] for number in rows_of]
+        )
 
     @pl.when(tx > 0)
     def _():
@@ -473,6 +475,20 @@
 
     for copy in (to_spec, to_wv, to_img, to_err):
         copy.wait_send()
+
+
+def write(scale, image, mask, errors, stats, image_out, mask_out, errors_out, peaks, shares, sems):
+    copies = [
+        pltpu.make_async_copy(src, dst, sems.at[i])
+        for i, (src, dst) in enumerate(((image, image_out), (mask, mask_out), (errors, errors_out)))
+    ]
+    for copy in copies:
+        copy.start()
+    for i in range(ITERS):
+        peaks[i] = jnp.max(stats[i : i + 1, :])
+        shares[i] = jnp.sum(stats[ITERS + i : ITERS + i + 1, :]) * scale
+    for copy in copies:
+        copy.wait()
 
 
 def shards(sizes, *args):
@@ -487,23 +503,25 @@
     vmem = pl.BlockSpec(memory_space=pltpu.VMEM)
     smem = pl.BlockSpec(memory_space=pltpu.SMEM)
     dma = pltpu.SemaphoreType.DMA
-    operands = (*args, *consts)
+    operands = tuple(
+        pltpu.with_memory_space_constraint(a, pltpu.HBM) for a in (*args, *consts)
+    )
     local = [
         (pltpu.SMEM if number in (9, 10) else pltpu.VMEM)(a.shape, a.dtype)
         for number, a in enumerate(operands)
     ]
-    return tuple(
-        pl.pallas_call(
+    tile_shape = (tile, tile)
+    error_shape = (1, 1, ITERS, site_count)
+    results = pl.pallas_call(
             functools.partial(kernel, sizes),
             out_shape=(
-                jax.ShapeDtypeStruct((tile, tile), F32),
-                jax.ShapeDtypeStruct((tile, tile), F32),
-                jax.ShapeDtypeStruct((1, 1, ITERS, site_count), F32),
-                jax.ShapeDtypeStruct((ITERS,), F32),
-                jax.ShapeDtypeStruct((ITERS,), F32),
+                pltpu.VMEM(tile_shape, F32),
+                pltpu.VMEM(tile_shape, F32),
+                pltpu.VMEM(error_shape, F32),
+                pltpu.VMEM((8, 128), F32),
             ),
             in_specs=[pl.BlockSpec(memory_space=pltpu.HBM)] * OPERANDS,
-            out_specs=(vmem, vmem, vmem, smem, smem),
+            out_specs=(vmem,) * 4,
             scratch_shapes=local
             + [
                 pltpu.VMEM((wide, tile), F32),
@@ -513,12 +531,13 @@
                 pltpu.VMEM((kernels, 128), F32),
                 pltpu.VMEM((2, BAND, BAND), F32),
                 pltpu.VMEM((tile, tile), F32),
+                pltpu.VMEM((tile, site_count), BF16),
                 pltpu.VMEM((tile, tile), F32),
                 pltpu.VMEM((tile, tile), F32),
                 pltpu.VMEM((1, site_count), F32),
                 pltpu.VMEM((1, site_count), F32),
-                pltpu.VMEM((8, 128), F32),
-                pltpu.VMEM((count, 8, 128), F32),
+                pltpu.VMEM((2, 128), F32),
+                pltpu.VMEM((count, 2, 128), F32),
                 dma((4,)),
                 dma((4,)),
                 dma((4,)),
@@ -528,9 +547,25 @@
                 dma((OPERANDS,)),
             ],
             compiler_params=pltpu.CompilerParams(
-                collective_id=0, has_side_effects=True
+                collective_id=0, has_side_effects=True, vmem_limit_bytes=VMEM_LIMIT
             ),
         )(*operands)
+    hbm = pl.BlockSpec(memory_space=pltpu.HBM)
+    return tuple(
+        pl.pallas_call(
+            functools.partial(write, 1.0 / (site_count * sizes[0] * sizes[1])),
+            out_shape=(
+                jax.ShapeDtypeStruct(tile_shape, F32),
+                jax.ShapeDtypeStruct(tile_shape, F32),
+                jax.ShapeDtypeStruct(error_shape, F32),
+                jax.ShapeDtypeStruct((ITERS,), F32),
+                jax.ShapeDtypeStruct((ITERS,), F32),
+            ),
+            in_specs=[vmem] * 4,
+            out_specs=(hbm, hbm, hbm, smem, smem),
+            scratch_shapes=[dma((3,))],
+            compiler_params=pltpu.CompilerParams(vmem_limit_bytes=VMEM_LIMIT),
+        )(*results)
     )
 
 

time: 34.8 us -> 30.2 us (0.87)
  local copies, waits for them, and re-layouts: 4.2 us -> 0 us
    unnamed x13 -> x0, local copies, waits for them, and re-layouts: 4.2 us -> none
    pallas_call x1 -> x2, Pallas kernels: 29.6 us -> 29.3 us  [the longest x1 28 us: shards(): pl.pallas_call(functools.partial(kernel, sizes), out_shape=(pltpu.VMEM(ti...]
where the time goes in v1:
time: 30.2 us; the launch traced here: 30 us
  Pallas kernels  29.3 us (97%)
  between operations  0.64 us (2%)
    pallas_call x1, Pallas kernels, shards(): pl.pallas_call(functools.partial(kernel, sizes), out_shape=(pltpu.VMEM(ti...  28 us
    pallas_call x1, Pallas kernels, shards(): pl.pallas_call(functools.partial(write, 1.0 / (site_count * sizes[0] * si...  1.35 us

profile of v1, /device:TPU:0, one launch (start us, length us, event | category | flops | bytes accessed | tf_op | source)
XLA Modules:
  0.0 30.0 jit_solution(10328298454390313199)
XLA Ops:
  0.6 28.0 %shard_map.209 = (f32[256,256]{1,0:T(8,128)S(1)}, f32[256,256]{1,0:T(8,128)S(1)}, f32[1,1,2,2048]{3,2,1,0:T(2,128)S(1)}, f32[8,128]{1,0:T(8,128)S(1)}) custom-call(f32[256,256]{1,0:T(8,128)} %refs_0_.1, s32[1,1,512]{2,1,0:T(1,128)} %refs_1_.1, s32[1,1,512]{2,1,0:T(1,128)} %refs_2_.1, s32[1,1,512]{2,1,0:T(1,128)} %refs_3_.1, s32[1,1,512]{2,1,0:T(1,128)} %refs_4_.1, ...), custom_call_target="tpu_custom_call" | custom-call | tf_op jit(solution)/shard_map/pallas_call | solution.py:515
  28.6 1.3 %shard_map.210 = (f32[256,256]{1,0:T(8,128)}, f32[256,256]{1,0:T(8,128)}, f32[1,1,2,2048]{3,2,1,0:T(2,128)}, f32[2]{0:T(128)}, f32[2]{0:T(128)}) custom-call(f32[256,256]{1,0:T(8,128)S(1)} %get-tuple-element.9.image, f32[256,256]{1,0:T(8,128)S(1)} %get-tuple-element.10.mask, f32[1,1,2,2048]{3,2,1,0:T(2,128)S(1)} %get-tuple-element.11.errors, ...), custom_call_target="tpu_custom_call" | custom-call | tf_op jit(solution)/shard_map/pallas_call | solution.py:555

commit v2 on v1

--- a/solution.py
+++ b/solution.py
@@ -171,11 +171,12 @@
     ka_recv,
     stat_send,
     stat_recv,
+    token,
 ):
     n_tx, n_ty, n_ka = sizes
     count = n_tx * n_ty * n_ka
     tile = mask_ref.shape[0]
-    wide = ext.shape[0]
+    wide = ext.shape[1]
     sites = srow_ref.shape[2]
     kernels = spec_ref.shape[0]
     group = lax.axis_index("groups")
@@ -200,45 +201,83 @@
     begin(1, 2, 3, 4, 5, 0, 9, 11, 12, 8, 13, 14, 15, 16, 17, 6, 7, 10)
     barrier = pltpu.get_barrier_semaphore()
 
-    def greet(offset, carry):
-        pl.semaphore_signal(
-            barrier, inc=1, device_id=place(lax.rem(me + offset, count)), device_id_type=MESH
-        )
-        return carry
-
-    lax.fori_loop(1, count, greet, 0)
-
-    need(1, 2, 3, 4, 5, 0)
-    fragments = (frow_ref[0], fcol_ref[0], flen_ref[0], fori_ref[0])
-    first = jnp.clip(mask_ref[...] + strip_sum(*fragments, fmove_ref[0, 0, 0:1, :], tile), 0.0, 1.0)
-    second = jnp.clip(first + strip_sum(*fragments, fmove_ref[0, 0, 1:2, :], tile), 0.0, 1.0)
-    mask_out_ref[...] = second
-    ext[HALO : HALO + tile, :] = jnp.where(ka == 0, first, second)
-    need(9)
-    for k in range(kernels):
-        wv[k : k + 1, :] = jnp.full((1, 128), weight_ref[k], F32)
-
-    pl.semaphore_wait(barrier, count - 1)
-
     partner = (group, tx, ty, 1 - ka)
     up = (group, tx - 1, ty, ka)
     down = (group, tx + 1, ty, ka)
     left = (group, tx, ty - 1, ka)
     right = (group, tx, ty + 1, ka)
-    to_up = remote(
-        ext.at[pl.ds(HALO, HALO)], ext.at[pl.ds(HALO + tile, HALO)], halo_send.at[0], halo_recv.at[0], up
-    )
-    to_down = remote(
-        ext.at[pl.ds(tile, HALO)], ext.at[pl.ds(0, HALO)], halo_send.at[1], halo_recv.at[1], down
-    )
-
-    @pl.when(tx > 0)
-    def _():
-        to_up.start()
-
-    @pl.when(tx < n_tx - 1)
-    def _():
-        to_down.start()
+    around = ((tx > 0, up), (tx < n_tx - 1, down), (ty > 0, left), (ty < n_ty - 1, right))
+
+    def signal(semaphore, target):
+        pl.semaphore_signal(semaphore, inc=1, device_id=target, device_id_type=MESH)
+
+    signal(barrier, partner)
+    for there, target in around:
+        pl.when(there)(functools.partial(signal, barrier, target))
+
+    need(1, 2, 3, 4, 5, 0)
+    fragments = (frow_ref[0], fcol_ref[0], flen_ref[0], fori_ref[0])
+    early = lax.div(n_ty - 1 - ty, max(n_ty - 1, 1))
+    halves = (early, 1 - early)
+
+    def to_up(half):
+        return remote(
+            ext.at[half, pl.ds(HALO, HALO)],
+            ext.at[half, pl.ds(HALO + tile, HALO)],
+            halo_send.at[half],
+            halo_recv.at[half],
+            up,
+        )
+
+    def to_down(half):
+        return remote(
+            ext.at[half, pl.ds(tile, HALO)],
+            ext.at[half, pl.ds(0, HALO)],
+            halo_send.at[2 + half],
+            halo_recv.at[2 + half],
+            down,
+        )
+
+    def chain(hop, at, count_at, before, after, previous, following):
+        if 0 < hop:
+            pl.when(at == hop)(lambda: pl.semaphore_wait(token.at[before], 1))
+            pl.when(at == count_at - 1 - hop)(lambda: pl.semaphore_wait(token.at[after], 1))
+        if hop < count_at - 1:
+            pl.when(at == hop)(lambda: signal(token.at[before], following))
+            pl.when(at == count_at - 1 - hop)(lambda: signal(token.at[after], previous))
+
+    def pass_across(hop):
+        chain(hop, ty, n_ty, 0, 1, left, right)
+
+    def pass_on(hop):
+        chain(hop, tx, n_tx, 2, 3, up, down)
+
+    def send_rows():
+        for half in halves:
+            pl.when(tx > 0)(lambda: to_up(half).start())
+            pl.when(tx < n_tx - 1)(lambda: to_down(half).start())
+
+    def place_rows(values):
+        for half in range(2):
+            ext[half, HALO : HALO + tile, :] = values[:, half * HALO : (half + 1) * HALO]
+
+    first = jnp.clip(mask_ref[...] + strip_sum(*fragments, fmove_ref[0, 0, 0:1, :], tile), 0.0, 1.0)
+    second = jnp.clip(first + strip_sum(*fragments, fmove_ref[0, 0, 1:2, :], tile), 0.0, 1.0)
+    mask_out_ref[...] = second
+    place_rows(jnp.where(ka == 0, first, second))
+
+    peers = 1
+    for at, count_at in ((tx, n_tx), (ty, n_ty)):
+        for steps in (at, count_at - 1 - at):
+            peers = peers + lax.div(steps + count_at - 1, count_at)
+    pl.semaphore_wait(barrier, peers)
+
+    send_rows()
+    pass_across(0)
+
+    need(9)
+    for k in range(kernels):
+        wv[k : k + 1, :] = jnp.full((1, 128), weight_ref[k], F32)
 
     to_spec = remote(spec_away, spec_rx, ka_send.at[0], ka_recv.at[0], partner)
     to_wv = remote(wv, wv_rx, ka_send.at[1], ka_recv.at[1], partner)
@@ -253,11 +292,11 @@
 
     @pl.when(tx == 0)
     def _():
-        ext[0:HALO, :] = jnp.zeros((HALO, tile), F32)
+        ext[:, 0:HALO, :] = jnp.zeros((2, HALO, HALO), F32)
 
     @pl.when(tx == n_tx - 1)
     def _():
-        ext[HALO + tile : wide, :] = jnp.zeros((HALO, tile), F32)
+        ext[:, HALO + tile : wide, :] = jnp.zeros((2, HALO, HALO), F32)
 
     @pl.when(ty == 0)
     def _():
@@ -266,44 +305,38 @@
     @pl.when(ty == n_ty - 1)
     def _():
         hext[3] = jnp.zeros(hext.shape[1:], F32)
-
-    @pl.when(tx > 0)
-    def _():
-        to_down.wait_recv()
-
-    @pl.when(tx < n_tx - 1)
-    def _():
-        to_up.wait_recv()
 
     rows = hext.shape[1]
     need(11)
-    high, middle, low = split3(ext[...])
-    by_high = dot(forward_ref[...], high)
-    by_middle = dot(forward_ref[0 : 2 * rows, :], middle)
-    by_low = dot(forward_ref[0:rows, :], low)
-    half = (by_low + by_high[2 * rows :] + by_middle[rows:]) + (by_high[rows : 2 * rows] + by_middle[:rows])
-    half = half + by_high[:rows]
-    hext[1] = half[:, :HALO]
-    hext[2] = half[:, HALO:]
-    to_left = remote(hext.at[1], hext.at[3], halo_send.at[2], halo_recv.at[2], left)
-    to_right = remote(hext.at[2], hext.at[0], halo_send.at[3], halo_recv.at[3], right)
+    to_left = remote(hext.at[1], hext.at[3], halo_send.at[4], halo_recv.at[4], left)
+    to_right = remote(hext.at[2], hext.at[0], halo_send.at[5], halo_recv.at[5], right)
+    for half in halves:
+        pl.when(tx > 0)(lambda: to_down(half).wait_recv())
+        pl.when(tx < n_tx - 1)(lambda: to_up(half).wait_recv())
+        high, middle, low = split3(ext[half])
+        by = dot(forward_ref[...], jnp.concatenate([high, middle], axis=1))
+        by_high, by_middle = by[:, :HALO], by[:, HALO:]
+        by_low = dot(forward_ref[0:rows, :], low)
+        total = (by_low + by_high[2 * rows :] + by_middle[rows : 2 * rows]) + (
+            by_high[rows : 2 * rows] + by_middle[:rows]
+        )
+        hext[1 + half] = total + by_high[:rows]
+        pl.when((half == 0) & (ty > 0))(to_left.start)
+        pl.when((half == 1) & (ty < n_ty - 1))(to_right.start)
+
+    for hop in range(1, n_ty):
+        pass_across(hop)
+    pass_on(0)
 
     @pl.when(ty > 0)
     def _():
-        to_left.start()
+        to_right.wait_recv()
 
     @pl.when(ty < n_ty - 1)
     def _():
-        to_right.start()
-
-    @pl.when(ty > 0)
-    def _():
-        to_right.wait_recv()
-
-    @pl.when(ty < n_ty - 1)
-    def _():
         to_left.wait_recv()
 
+    pass_on(1)
     need(12, 13)
     whole = jnp.concatenate([hext[0], hext[1], hext[2], hext[3]], axis=1)
     high, middle, low = split3(whole)
@@ -373,12 +406,15 @@
     lax.fori_loop(0, kernels // 4, own_step, 0)
     for k in range(kernels // 4 * 4, kernels):
         add_one(spec_ref, wv, k)
+    pass_on(2)
     to_spec.wait_recv()
     to_wv.wait_recv()
     lax.fori_loop(0, kernels // 4, rx_step, 0)
     for k in range(kernels // 4 * 4, kernels):
         add_one(spec_rx, wv_rx, k)
 
+    for hop in range(3, n_tx):
+        pass_on(hop)
     need(16, 17)
     lower = jnp.concatenate(split3(folded[mid:, :]), axis=0)
     ordered = jnp.concatenate([dot(flip_wide_ref[...], lower), folded[:mid, :]], axis=0)
@@ -457,13 +493,9 @@
             jnp.add, [stat_rx[number, 1:2, :] for number in rows_of]
         )
 
-    @pl.when(tx > 0)
-    def _():
-        to_up.wait_send()
-
-    @pl.when(tx < n_tx - 1)
-    def _():
-        to_down.wait_send()
+    for half in range(2):
+        pl.when(tx > 0)(lambda: to_up(half).wait_send())
+        pl.when(tx < n_tx - 1)(lambda: to_down(half).wait_send())
 
     @pl.when(ty > 0)
     def _():
@@ -524,7 +556,7 @@
             out_specs=(vmem,) * 4,
             scratch_shapes=local
             + [
-                pltpu.VMEM((wide, tile), F32),
+                pltpu.VMEM((2, wide, HALO), F32),
                 pltpu.VMEM((4, rows, HALO), F32),
                 pltpu.VMEM(spectra.shape, F32),
                 pltpu.VMEM((kernels, 128), F32),
@@ -538,12 +570,13 @@
                 pltpu.VMEM((1, site_count), F32),
                 pltpu.VMEM((2, 128), F32),
                 pltpu.VMEM((count, 2, 128), F32),
-                dma((4,)),
-                dma((4,)),
+                dma((6,)),
+                dma((6,)),
                 dma((4,)),
                 dma((4,)),
                 dma((count,)),
                 dma((count,)),
+                pltpu.SemaphoreType.REGULAR((4,)),
                 dma((OPERANDS,)),
             ],
             compiler_params=pltpu.CompilerParams(

time: 30.2 us -> 28.1 us (0.930)
  Pallas kernels: 29.3 us -> 27.3 us
    pallas_call x1, Pallas kernels: 28 us -> 26 us  [shards(): pl.pallas_call(functools.partial(kernel, sizes), out_shape=(pltpu.VMEM(ti...]
where the time goes in v2:
time: 28.1 us; the launch traced here: 28 us
  Pallas kernels  27.3 us (97%)
  between operations  0.64 us (2%)
    pallas_call x1, Pallas kernels, shards(): pl.pallas_call(functools.partial(kernel, sizes), out_shape=(pltpu.VMEM(ti...  26 us
    pallas_call x1, Pallas kernels, shards(): pl.pallas_call(functools.partial(write, 1.0 / (site_count * sizes[0] * si...  1.35 us

profile of v2, /device:TPU:0, one launch (start us, length us, event | category | flops | bytes accessed | tf_op | source)
XLA Modules:
  0.0 28.0 jit_solution(14023893289753586217)
XLA Ops:
  0.6 26.0 %shard_map.209 = (f32[256,256]{1,0:T(8,128)S(1)}, f32[256,256]{1,0:T(8,128)S(1)}, f32[1,1,2,2048]{3,2,1,0:T(2,128)S(1)}, f32[8,128]{1,0:T(8,128)S(1)}) custom-call(f32[256,256]{1,0:T(8,128)} %refs_0_.1, s32[1,1,512]{2,1,0:T(1,128)} %refs_1_.1, s32[1,1,512]{2,1,0:T(1,128)} %refs_2_.1, s32[1,1,512]{2,1,0:T(1,128)} %refs_3_.1, s32[1,1,512]{2,1,0:T(1,128)} %refs_4_.1, ...), custom_call_target="tpu_custom_call" | custom-call | tf_op jit(solution)/shard_map/pallas_call | solution.py:547
  26.6 1.3 %shard_map.210 = (f32[256,256]{1,0:T(8,128)}, f32[256,256]{1,0:T(8,128)}, f32[1,1,2,2048]{3,2,1,0:T(2,128)}, f32[2]{0:T(128)}, f32[2]{0:T(128)}) custom-call(f32[256,256]{1,0:T(8,128)S(1)} %get-tuple-element.9.image, f32[256,256]{1,0:T(8,128)S(1)} %get-tuple-element.10.mask, f32[1,1,2,2048]{3,2,1,0:T(2,128)S(1)} %get-tuple-element.11.errors, ...), custom_call_target="tpu_custom_call" | custom-call | tf_op jit(solution)/shard_map/pallas_call | solution.py:588

commit v3 on v2

--- a/solution.py
+++ b/solution.py
@@ -18,7 +18,8 @@
 SLOPE_FLOOR = 0.05
 SHARPNESS = 8.0
 CHUNK = 256
-OPERANDS = 18
+ROWS = 32
+OPERANDS = 19
 VMEM_LIMIT = 32 * 1024 * 1024
 MESH = pl.DeviceIdType.MESH
 F32 = jnp.float32
@@ -44,21 +45,33 @@
     forward = np.zeros((rows, ext))
     forward[: half + 1] = np.cos(step * positive[:, None] * span[None])
     forward[half + 1 : 2 * half + 1] = np.sin(step * positive[1:, None] * span[None])
-    phase = step * span[:, None] * freq[None]
+    pairs = np.arange(half)
+    phase = step * span[:, None] * np.concatenate([pairs, -1 - pairs])[None]
     across = np.concatenate([np.cos(phase), np.sin(phase)], axis=1)
+    across = np.concatenate([across[HALO:-HALO], across[:HALO], across[-HALO:]], axis=0)
     expand = np.zeros((2 * BAND, 2 * BAND))
     for place, number in enumerate(freq):
         expand[place, abs(number)] = 1.0
         if number != 0:
             expand[BAND + place, half + abs(number)] = np.sign(number)
-    angle = step * (np.arange(tile // 2)[:, None] + 0.5) * freq[None]
+    pixels = np.arange(tile // 2) + 0.5
+    angle = step * pixels[:, None] * (freq[None] + 0.5)
     back_rows = np.concatenate([np.cos(angle), np.sin(angle)], axis=0) / ext
-    back_cols = np.concatenate([np.cos(angle.T), np.sin(angle.T)], axis=1) / ext
+    angle = step * (pairs[:, None] + 0.5) * pixels[None]
+    turn = np.eye(half)[::-1]
+    turn = np.block([[turn, 0 * turn], [0 * turn, turn]]).astype(ml_dtypes.bfloat16)
     flip = np.eye(tile // 2)[::-1].astype(ml_dtypes.bfloat16)
     high, middle, low = pieces_of(back_rows)
     rows6 = np.concatenate([high, high, middle, high, middle, low], axis=1)
-    high, middle, low = pieces_of(back_cols)
-    cols6 = np.concatenate([high, high, middle, high, middle, low], axis=0)
+    cols6 = []
+    for wave in (np.cos(angle), np.sin(angle)):
+        high, middle, low = pieces_of(wave / ext)
+        none = np.zeros_like(high)
+        cols6.append(np.concatenate([high, high, high, low], axis=0))
+        cols6.append(np.concatenate([middle, middle, none, none], axis=0))
+    cols6 = np.concatenate(
+        [np.concatenate(cols6[:2], axis=1), np.concatenate(cols6[2:], axis=1)], axis=0
+    )
     return (
         np.concatenate(pieces_of(forward), axis=0),
         np.concatenate(pieces_of(across), axis=0),
@@ -67,6 +80,7 @@
         cols6,
         np.concatenate([flip] * 3, axis=1),
         np.concatenate([flip] * 3, axis=0),
+        np.concatenate([turn] * 3, axis=0),
     )
 
 
@@ -121,14 +135,13 @@
         for number in numbers:
             copies[number].start()
 
-    body(sizes, start, need, away[8], *here, *outs, *rest[:-1])
+    body(sizes, start, need, *here, *outs, *rest[:-1])
 
 
 def body(
     sizes,
     begin,
     need,
-    spec_away,
     mask_ref,
     frow_ref,
     fcol_ref,
@@ -147,15 +160,16 @@
     cols_ref,
     flip_wide_ref,
     flip_tall_ref,
+    turn_ref,
     intensity_ref,
     mask_out_ref,
     errors_ref,
     stats_ref,
     ext,
     hext,
-    spec_rx,
-    wv,
-    wv_rx,
+    paired,
+    stacked_a,
+    stacked_b,
     sbuf,
     folded,
     choose,
@@ -198,7 +212,7 @@
             src_ref=src, dst_ref=dst, send_sem=send, recv_sem=recv, device_id=target, device_id_type=MESH
         )
 
-    begin(1, 2, 3, 4, 5, 0, 9, 11, 12, 8, 13, 14, 15, 16, 17, 6, 7, 10)
+    begin(1, 2, 3, 4, 5, 0, 9, 7, 18, 8, 11, 12, 13, 14, 15, 6, 10, 16, 17)
     barrier = pltpu.get_barrier_semaphore()
 
     partner = (group, tx, ty, 1 - ka)
@@ -261,34 +275,53 @@
         for half in range(2):
             ext[half, HALO : HALO + tile, :] = values[:, half * HALO : (half + 1) * HALO]
 
-    first = jnp.clip(mask_ref[...] + strip_sum(*fragments, fmove_ref[0, 0, 0:1, :], tile), 0.0, 1.0)
-    second = jnp.clip(first + strip_sum(*fragments, fmove_ref[0, 0, 1:2, :], tile), 0.0, 1.0)
-    mask_out_ref[...] = second
-    place_rows(jnp.where(ka == 0, first, second))
-
     peers = 1
     for at, count_at in ((tx, n_tx), (ty, n_ty)):
         for steps in (at, count_at - 1 - at):
             peers = peers + lax.div(steps + count_at - 1, count_at)
-    pl.semaphore_wait(barrier, peers)
-
-    send_rows()
-    pass_across(0)
-
-    need(9)
-    for k in range(kernels):
-        wv[k : k + 1, :] = jnp.full((1, 128), weight_ref[k], F32)
-
-    to_spec = remote(spec_away, spec_rx, ka_send.at[0], ka_recv.at[0], partner)
-    to_wv = remote(wv, wv_rx, ka_send.at[1], ka_recv.at[1], partner)
-    to_spec.start()
-    to_wv.start()
+
+    def send_off():
+        pl.semaphore_wait(barrier, peers)
+        send_rows()
+        pass_across(0)
+
+    first = jnp.clip(mask_ref[...] + strip_sum(*fragments, fmove_ref[0, 0, 0:1, :], tile), 0.0, 1.0)
+    place_rows(first)
+    second = jnp.clip(first + strip_sum(*fragments, fmove_ref[0, 0, 1:2, :], tile), 0.0, 1.0)
+    mask_out_ref[...] = second
+    pl.when(ka == 1)(lambda: place_rows(second))
+    send_off()
+
+    def fold(at):
+        return jnp.where(at < tile // 2, tile - 1 - at, at - tile // 2)
 
     need(7)
     position = lax.broadcasted_iota(jnp.int32, (tile, CHUNK), 0)
     for start in range(0, sites, CHUNK):
-        at_cols = scol_ref[0, :, start : start + CHUNK]
+        at_cols = fold(scol_ref[0, :, start : start + CHUNK])
         choose[:, start : start + CHUNK] = jnp.where(position == at_cols, 1.0, 0.0).astype(BF16)
+
+    lower_lanes = lax.broadcasted_iota(jnp.int32, (BAND, BAND), 1) < BAND // 2
+
+    def swap(value):
+        return pltpu.roll(value, BAND // 2, 1)
+
+    def pair(k):
+        scale = jnp.sqrt(jnp.full((1, BAND), weight_ref[k], F32))
+        k_re, k_im = spec_ref[k, 0], spec_ref[k, 1]
+        below = jnp.where(lower_lanes, k_re, swap(k_im)) * scale
+        paired[k, 0] = jnp.where(lower_lanes, swap(k_re), k_im) * scale
+        paired[k, 1] = dot(jnp.concatenate(split3(below), axis=1), turn_ref[...])
+
+    def pair_step(k, carry):
+        for number in range(4):
+            pair(4 * k + number)
+        return carry
+
+    need(9, 8, 18)
+    lax.fori_loop(0, kernels // 4, pair_step, 0)
+    for k in range(kernels // 4 * 4, kernels):
+        pair(k)
 
     @pl.when(tx == 0)
     def _():
@@ -326,7 +359,33 @@
 
     for hop in range(1, n_ty):
         pass_across(hop)
+    to_spec = remote(
+        paired.at[pl.ds(0, kernels)],
+        paired.at[pl.ds(kernels, kernels)],
+        ka_send.at[0],
+        ka_recv.at[0],
+        partner,
+    )
+    to_spec.start()
     pass_on(0)
+    need(12, 13)
+
+    def column_part(block, first_row):
+        high, middle, low = split3(block)
+        depth = block.shape[1]
+
+        def piece(number):
+            return across_ref[number * wide + first_row : number * wide + first_row + depth, :]
+
+        by_high = dot(jnp.concatenate([high, middle, low], axis=0), piece(0))
+        by_middle = dot(jnp.concatenate([high, middle], axis=0), piece(1))
+        by_low = dot(high, piece(2))
+        part = (by_low + by_high[2 * rows :] + by_middle[rows:]) + (
+            by_high[rows : 2 * rows] + by_middle[:rows]
+        )
+        return part + by_high[:rows]
+
+    own_part = column_part(jnp.concatenate([hext[1], hext[2]], axis=1), 0)
 
     @pl.when(ty > 0)
     def _():
@@ -337,95 +396,98 @@
         to_left.wait_recv()
 
     pass_on(1)
-    need(12, 13)
-    whole = jnp.concatenate([hext[0], hext[1], hext[2], hext[3]], axis=1)
-    high, middle, low = split3(whole)
-    by_high = dot(jnp.concatenate([high, middle, low], axis=0), across_ref[0:wide, :])
-    by_middle = dot(jnp.concatenate([high, middle], axis=0), across_ref[wide : 2 * wide, :])
-    by_low = dot(high, across_ref[2 * wide :, :])
-    full = (by_low + by_high[2 * rows :] + by_middle[rows:]) + (by_high[rows : 2 * rows] + by_middle[:rows])
-    full = full + by_high[:rows]
+    full = own_part + column_part(jnp.concatenate([hext[0], hext[3]], axis=1), tile)
     full = jnp.concatenate([full, jnp.zeros((2 * BAND - rows, 2 * BAND), F32)], axis=0)
     mixed = dot(expand_ref[...], jnp.concatenate(split3(full), axis=0))
-    sbuf[0] = mixed[:BAND, :BAND] - mixed[BAND:, BAND:]
-    sbuf[1] = -(mixed[BAND:, :BAND] + mixed[:BAND, BAND:])
+    s_re = mixed[:BAND, :BAND] - mixed[BAND:, BAND:]
+    s_im = -(mixed[BAND:, :BAND] + mixed[:BAND, BAND:])
+    sbuf[0] = jnp.where(lower_lanes, s_re, swap(s_re))
+    sbuf[1] = jnp.where(lower_lanes, -s_im, swap(s_im))
+    sbuf[2] = jnp.where(lower_lanes, swap(s_re), s_re)
+    sbuf[3] = jnp.where(lower_lanes, -swap(s_im), s_im)
 
     mid = tile // 2
     folded[...] = jnp.zeros_like(folded)
 
-    def kernel_image(spectra, scales, k):
-        scale = jnp.sqrt(scales[pl.ds(k, 1), :])
-        k_re = spectra[k, 0] * scale
-        k_im = spectra[k, 1] * scale
-        s_re = sbuf[0]
-        s_im = sbuf[1]
-        p_re = k_re * s_re - k_im * s_im
-        p_im = k_re * s_im + k_im * s_re
-        high, middle, low = split3(jnp.concatenate([p_re, p_im], axis=1))
-        parts = dot(
+    low_half = lax.broadcasted_iota(jnp.int32, (tile, BAND), 1) < BAND // 2
+
+    def first_stage(k, stacked):
+        plus, minus = paired[k, 0], paired[k, 1]
+        p_plus = plus * sbuf[0] + swap(plus) * sbuf[1]
+        p_minus = minus * sbuf[2] + swap(minus) * sbuf[3]
+        high, middle, low = split3(
+            jnp.concatenate([p_plus + p_minus, p_plus - p_minus], axis=1)
+        )
+        inner = dot(
             rows_ref[...], jnp.concatenate([high, middle, high, low, middle, high], axis=0)
         )
-        even_re, even_im = parts[:mid, :BAND], parts[:mid, BAND:]
-        odd_re, odd_im = parts[mid:, :BAND], parts[mid:, BAND:]
-        inner = jnp.concatenate(
-            [even_re - odd_im, even_re + odd_im, even_im + odd_re, even_im - odd_re], axis=0
-        )
-        high, middle, low = split3(inner)
+        for number in range(2):
+            part = inner[:, number * BAND : (number + 1) * BAND]
+            high, middle, low = split3(part)
+            high_turned, middle_turned, low_turned = swap(high), swap(middle), swap(low)
+            blocks = (
+                (jnp.where(low_half, high, middle_turned), jnp.where(low_half, low, high_turned)),
+                (jnp.where(low_half, high_turned, middle), jnp.where(low_half, low_turned, high)),
+            )
+            for row in range(0, mid, ROWS):
+                for place_in, (left_part, right_part) in enumerate(blocks):
+                    for wave in range(2):
+                        at = 4 * row + (2 * place_in + wave) * ROWS
+                        taken = slice(wave * mid + row, wave * mid + row + ROWS)
+                        stacked[number, at : at + ROWS, :BAND] = left_part[taken]
+                        stacked[number, at : at + ROWS, BAND:] = right_part[taken]
+
+    def across_part(stacked, number, row):
         turned = dot(
-            jnp.concatenate([high, middle, high, low, middle, high], axis=1), cols_ref[...]
-        )
-        re_cos, re_sin = turned[:tile, :mid], turned[:tile, mid:]
-        im_cos, im_sin = turned[tile:, :mid], turned[tile:, mid:]
-        f_re, f_im = re_cos - im_sin, im_cos + re_sin
-        near = f_re * f_re + f_im * f_im
-        f_re, f_im = re_cos + im_sin, im_cos - re_sin
-        return near, f_re * f_re + f_im * f_im
-
-    def add_pair(spectra, scales, k):
-        near_a, far_a = kernel_image(spectra, scales, 4 * k)
-        near_b, far_b = kernel_image(spectra, scales, 4 * k + 1)
-        near_c, far_c = kernel_image(spectra, scales, 4 * k + 2)
-        near_d, far_d = kernel_image(spectra, scales, 4 * k + 3)
-        folded[:, :mid] += (near_a + near_b) + (near_c + near_d)
-        folded[:, mid:] += (far_a + far_b) + (far_c + far_d)
-
-    def add_one(spectra, scales, k):
-        near, far = kernel_image(spectra, scales, k)
-        folded[:, :mid] += near
-        folded[:, mid:] += far
-
-    def own_step(k, carry):
-        add_pair(spec_ref, wv, k)
+            stacked[number, 4 * row : 4 * (row + ROWS), :],
+            cols_ref[number * tile : (number + 1) * tile, :],
+        )
+        whole = turned[:, :mid] + turned[:, mid:]
+        return [whole[quarter * ROWS : (quarter + 1) * ROWS] for quarter in range(4)]
+
+    def second_stage(stacked):
+        for row in range(0, mid, ROWS):
+            cc_re, sc_re, cc_im, sc_im = across_part(stacked, 0, row)
+            cs_re, ss_re, cs_im, ss_im = across_part(stacked, 1, row)
+
+            def both(side, x_re, x_im, y_re, y_im):
+                at = (slice(row, row + ROWS), slice(side, side + mid))
+                folded[at] += (x_re - y_im) * (x_re - y_im) + (x_im + y_re) * (x_im + y_re)
+                at = (slice(mid + row, mid + row + ROWS), slice(mid - side, tile - side))
+                folded[at] += (x_re + y_im) * (x_re + y_im) + (x_im - y_re) * (x_im - y_re)
+
+            both(0, cc_re - ss_re, cc_im - ss_im, sc_re + cs_re, sc_im + cs_im)
+            both(mid, cc_re + ss_re, cc_im + ss_im, sc_re - cs_re, sc_im - cs_im)
+
+    stacks = (stacked_a, stacked_b)
+    unroll = 4 if kernels % 2 == 0 else 2
+
+    def some_kernels(k, carry):
+        for number in range(unroll):
+            following = jnp.minimum(unroll * k + number + 1, 2 * kernels - 1)
+            first_stage(following, stacks[(number + 1) % 2])
+            second_stage(stacks[number % 2])
         return carry
 
-    def rx_step(k, carry):
-        add_pair(spec_rx, wv_rx, k)
-        return carry
-
-    need(8, 14, 15)
-    lax.fori_loop(0, kernels // 4, own_step, 0)
-    for k in range(kernels // 4 * 4, kernels):
-        add_one(spec_ref, wv, k)
+    need(14, 15)
+    first_stage(0, stacked_a)
+    half_way = (kernels - 1) // unroll
+    lax.fori_loop(0, half_way, some_kernels, 0)
     pass_on(2)
     to_spec.wait_recv()
-    to_wv.wait_recv()
-    lax.fori_loop(0, kernels // 4, rx_step, 0)
-    for k in range(kernels // 4 * 4, kernels):
-        add_one(spec_rx, wv_rx, k)
-
+    lax.fori_loop(half_way, 2 * kernels // unroll, some_kernels, 0)
     for hop in range(3, n_tx):
         pass_on(hop)
-    need(16, 17)
-    lower = jnp.concatenate(split3(folded[mid:, :]), axis=0)
-    ordered = jnp.concatenate([dot(flip_wide_ref[...], lower), folded[:mid, :]], axis=0)
-    lower = jnp.concatenate(split3(ordered[:, mid:]), axis=1)
-    img[...] = jnp.concatenate([dot(lower, flip_tall_ref[...]), ordered[:, :mid]], axis=1)
-    to_img = remote(img, img_rx, ka_send.at[2], ka_recv.at[2], partner)
-    to_img.start()
-
-    image = img[...]
-    grad_rows = (pltpu.roll(image, tile - 1, 0) - pltpu.roll(image, 1, 0)) * 0.5
-    grad_cols = (pltpu.roll(image, tile - 1, 1) - pltpu.roll(image, 1, 1)) * 0.5
+    image = folded[...]
+
+    def gradient(axis):
+        along = lax.broadcasted_iota(jnp.int32, (tile, tile), axis)
+        before = jnp.where(
+            lax.rem(along, mid) == 0, pltpu.roll(image, mid, axis), pltpu.roll(image, 1, axis)
+        )
+        return (pltpu.roll(image, tile - 1, axis) - before) * 0.5
+
+    grad_rows, grad_cols = gradient(0), gradient(1)
     slope = jnp.sqrt(grad_rows * grad_rows + grad_cols * grad_cols)
     error_map = (image - LEVEL) / jnp.maximum(slope, SLOPE_FLOOR)
     high, low = split(error_map)
@@ -434,7 +496,7 @@
     peak = jnp.zeros((1, CHUNK), F32)
     total = jnp.zeros((1, CHUNK), F32)
     for start in range(0, sites, CHUNK):
-        at_rows = srow_ref[0, :, start : start + CHUNK]
+        at_rows = fold(srow_ref[0, :, start : start + CHUNK])
         picked = dot(high, choose[:, start : start + CHUNK]) + dot(low, choose[:, start : start + CHUNK])
         errors = jnp.sum(jnp.where(position == at_rows, picked, 0.0), axis=0, keepdims=True)
         err[:, start : start + CHUNK] = errors
@@ -466,8 +528,24 @@
     lax.fori_loop(1, count, send_stat, 0)
     stat_rx[pl.ds(me, 1)] = stat[...][None]
 
-    to_img.wait_recv()
-    intensity_ref[...] = jnp.where(ka == ITERS - 1, image, img_rx[...])
+    to_img = remote(img, img_rx, ka_send.at[2], ka_recv.at[2], partner)
+    need(16, 17)
+
+    @pl.when(ka == ITERS - 1)
+    def _():
+        lower = jnp.concatenate(split3(folded[mid:, :]), axis=0)
+        ordered = jnp.concatenate([dot(flip_wide_ref[...], lower), folded[:mid, :]], axis=0)
+        lower = jnp.concatenate(split3(ordered[:, mid:]), axis=1)
+        result = jnp.concatenate([dot(lower, flip_tall_ref[...]), ordered[:, :mid]], axis=1)
+        img[...] = result
+        to_img.start()
+        intensity_ref[...] = result
+
+    @pl.when(ka < ITERS - 1)
+    def _():
+        to_img.wait_recv()
+        intensity_ref[...] = img_rx[...]
+
     to_err.wait_recv()
     mine = err[...]
     theirs = err_rx[...]
@@ -505,7 +583,8 @@
     def _():
         to_right.wait_send()
 
-    for copy in (to_spec, to_wv, to_img, to_err):
+    pl.when(ka == ITERS - 1)(to_img.wait_send)
+    for copy in (to_spec, to_err):
         copy.wait_send()
 
 
@@ -558,10 +637,10 @@
             + [
                 pltpu.VMEM((2, wide, HALO), F32),
                 pltpu.VMEM((4, rows, HALO), F32),
-                pltpu.VMEM(spectra.shape, F32),
-                pltpu.VMEM((kernels, 128), F32),
-                pltpu.VMEM((kernels, 128), F32),
-                pltpu.VMEM((2, BAND, BAND), F32),
+                pltpu.VMEM((2 * kernels, *spectra.shape[1:]), F32),
+                pltpu.VMEM((2, 2 * tile, tile), BF16),
+                pltpu.VMEM((2, 2 * tile, tile), BF16),
+                pltpu.VMEM((4, BAND, BAND), F32),
                 pltpu.VMEM((tile, tile), F32),
                 pltpu.VMEM((tile, site_count), BF16),
                 pltpu.VMEM((tile, tile), F32),

time: 28.1 us -> 26.9 us (0.957)
  Pallas kernels: 27.3 us -> 26.1 us
    pallas_call x1, Pallas kernels: 26 us -> 24.7 us  [shards(): pl.pallas_call(functools.partial(kernel, sizes), out_shape=(pltpu.VMEM(ti...]
where the time goes in v3:
time: 26.9 us; the launch traced here: 26.7 us
  Pallas kernels  26.1 us (97%)
  between operations  0.64 us (2%)
    pallas_call x1, Pallas kernels, shards(): pl.pallas_call(functools.partial(kernel, sizes), out_shape=(pltpu.VMEM(ti...  24.7 us
    pallas_call x1, Pallas kernels, shards(): pl.pallas_call(functools.partial(write, 1.0 / (site_count * sizes[0] * si...  1.35 us

profile of v3, /device:TPU:0, one launch (start us, length us, event | category | flops | bytes accessed | tf_op | source)
XLA Modules:
  0.0 26.7 jit_solution(17038075408822856442)
XLA Ops:
  0.6 24.7 %shard_map.218 = (f32[256,256]{1,0:T(8,128)S(1)}, f32[256,256]{1,0:T(8,128)S(1)}, f32[1,1,2,2048]{3,2,1,0:T(2,128)S(1)}, f32[8,128]{1,0:T(8,128)S(1)}) custom-call(f32[256,256]{1,0:T(8,128)} %refs_0_.1, s32[1,1,512]{2,1,0:T(1,128)} %refs_1_.1, s32[1,1,512]{2,1,0:T(1,128)} %refs_2_.1, s32[1,1,512]{2,1,0:T(1,128)} %refs_3_.1, s32[1,1,512]{2,1,0:T(1,128)} %refs_4_.1, ...), custom_call_target="tpu_custom_call" | custom-call | tf_op jit(solution)/shard_map/pallas_call | solution.py:626
  25.4 1.3 %shard_map.219 = (f32[256,256]{1,0:T(8,128)}, f32[256,256]{1,0:T(8,128)}, f32[1,1,2,2048]{3,2,1,0:T(2,128)}, f32[2]{0:T(128)}, f32[2]{0:T(128)}) custom-call(f32[256,256]{1,0:T(8,128)S(1)} %get-tuple-element.9.image, f32[256,256]{1,0:T(8,128)S(1)} %get-tuple-element.10.mask, f32[1,1,2,2048]{3,2,1,0:T(2,128)S(1)} %get-tuple-element.11.errors, ...), custom_call_target="tpu_custom_call" | custom-call | tf_op jit(solution)/shard_map/pallas_call | solution.py:667

commit v4 on v3

--- a/solution.py
+++ b/solution.py
@@ -19,6 +19,7 @@
 SHARPNESS = 8.0
 CHUNK = 256
 ROWS = 32
+UNROLL = 4
 OPERANDS = 19
 VMEM_LIMIT = 32 * 1024 * 1024
 MESH = pl.DeviceIdType.MESH
@@ -407,14 +408,21 @@
     sbuf[3] = jnp.where(lower_lanes, -swap(s_im), s_im)
 
     mid = tile // 2
-    folded[...] = jnp.zeros_like(folded)
+    folded[0] = jnp.zeros(folded.shape[1:], F32)
+
+    to_sbuf = remote(
+        sbuf.at[pl.ds(0, 4)], sbuf.at[pl.ds(4, 4)], ka_send.at[1], ka_recv.at[1], partner
+    )
+    pl.when(ka == 0)(to_sbuf.start)
+    to_share = remote(folded.at[1], folded.at[1], ka_send.at[4], ka_recv.at[4], partner)
 
     low_half = lax.broadcasted_iota(jnp.int32, (tile, BAND), 1) < BAND // 2
 
-    def first_stage(k, stacked):
+    def first_stage(k, stacked, slot=0):
+        first = 4 * slot
         plus, minus = paired[k, 0], paired[k, 1]
-        p_plus = plus * sbuf[0] + swap(plus) * sbuf[1]
-        p_minus = minus * sbuf[2] + swap(minus) * sbuf[3]
+        p_plus = plus * sbuf[first] + swap(plus) * sbuf[first + 1]
+        p_minus = minus * sbuf[first + 2] + swap(minus) * sbuf[first + 3]
         high, middle, low = split3(
             jnp.concatenate([p_plus + p_minus, p_plus - p_minus], axis=1)
         )
@@ -445,40 +453,63 @@
         whole = turned[:, :mid] + turned[:, mid:]
         return [whole[quarter * ROWS : (quarter + 1) * ROWS] for quarter in range(4)]
 
-    def second_stage(stacked):
+    def second_stage(stacked, slot=0):
         for row in range(0, mid, ROWS):
             cc_re, sc_re, cc_im, sc_im = across_part(stacked, 0, row)
             cs_re, ss_re, cs_im, ss_im = across_part(stacked, 1, row)
 
             def both(side, x_re, x_im, y_re, y_im):
-                at = (slice(row, row + ROWS), slice(side, side + mid))
+                at = (slot, slice(row, row + ROWS), slice(side, side + mid))
                 folded[at] += (x_re - y_im) * (x_re - y_im) + (x_im + y_re) * (x_im + y_re)
-                at = (slice(mid + row, mid + row + ROWS), slice(mid - side, tile - side))
+                at = (slot, slice(mid + row, mid + row + ROWS), slice(mid - side, tile - side))
                 folded[at] += (x_re + y_im) * (x_re + y_im) + (x_im - y_re) * (x_im - y_re)
 
             both(0, cc_re - ss_re, cc_im - ss_im, sc_re + cs_re, sc_im + cs_im)
             both(mid, cc_re + ss_re, cc_im + ss_im, sc_re - cs_re, sc_im - cs_im)
 
     stacks = (stacked_a, stacked_b)
-    unroll = 4 if kernels % 2 == 0 else 2
+    shared = 2 * kernels - UNROLL
+    assert shared % UNROLL == 0 and kernels >= UNROLL
 
     def some_kernels(k, carry):
-        for number in range(unroll):
-            following = jnp.minimum(unroll * k + number + 1, 2 * kernels - 1)
+        for number in range(UNROLL):
+            following = jnp.minimum(UNROLL * k + number + 1, shared - 1)
             first_stage(following, stacks[(number + 1) % 2])
             second_stage(stacks[number % 2])
         return carry
 
+    def last_kernels(part, carry):
+        first, slot = kernels - UNROLL + kernels * part, 1 - part
+        first_stage(first, stacks[0], slot)
+        for number in range(UNROLL):
+            if number < UNROLL - 1:
+                first_stage(first + number + 1, stacks[(number + 1) % 2], slot)
+            second_stage(stacks[number % 2], slot)
+        pl.when(part == 0)(to_share.start)
+        return carry
+
     need(14, 15)
     first_stage(0, stacked_a)
-    half_way = (kernels - 1) // unroll
+    half_way = (kernels - 1) // UNROLL
     lax.fori_loop(0, half_way, some_kernels, 0)
     pass_on(2)
     to_spec.wait_recv()
-    lax.fori_loop(half_way, 2 * kernels // unroll, some_kernels, 0)
+    lax.fori_loop(half_way, shared // UNROLL, some_kernels, 0)
+
+    @pl.when(ka == 1)
+    def _():
+        folded[1] = jnp.zeros(folded.shape[1:], F32)
+        to_sbuf.wait_recv()
+        lax.fori_loop(0, 2, last_kernels, 0)
+
+    @pl.when(ka == 0)
+    def _():
+        to_share.wait_recv()
+        folded[0] += folded[1]
+
     for hop in range(3, n_tx):
         pass_on(hop)
-    image = folded[...]
+    image = folded[0]
 
     def gradient(axis):
         along = lax.broadcasted_iota(jnp.int32, (tile, tile), axis)
@@ -533,8 +564,8 @@
 
     @pl.when(ka == ITERS - 1)
     def _():
-        lower = jnp.concatenate(split3(folded[mid:, :]), axis=0)
-        ordered = jnp.concatenate([dot(flip_wide_ref[...], lower), folded[:mid, :]], axis=0)
+        lower = jnp.concatenate(split3(folded[0, mid:, :]), axis=0)
+        ordered = jnp.concatenate([dot(flip_wide_ref[...], lower), folded[0, :mid, :]], axis=0)
         lower = jnp.concatenate(split3(ordered[:, mid:]), axis=1)
         result = jnp.concatenate([dot(lower, flip_tall_ref[...]), ordered[:, :mid]], axis=1)
         img[...] = result
@@ -584,6 +615,8 @@
         to_right.wait_send()
 
     pl.when(ka == ITERS - 1)(to_img.wait_send)
+    pl.when(ka == 0)(to_sbuf.wait_send)
+    pl.when(ka == 1)(to_share.wait_send)
     for copy in (to_spec, to_err):
         copy.wait_send()
 
@@ -640,8 +673,8 @@
                 pltpu.VMEM((2 * kernels, *spectra.shape[1:]), F32),
                 pltpu.VMEM((2, 2 * tile, tile), BF16),
                 pltpu.VMEM((2, 2 * tile, tile), BF16),
-                pltpu.VMEM((4, BAND, BAND), F32),
-                pltpu.VMEM((tile, tile), F32),
+                pltpu.VMEM((8, BAND, BAND), F32),
+                pltpu.VMEM((2, tile, tile), F32),
                 pltpu.VMEM((tile, site_count), BF16),
                 pltpu.VMEM((tile, tile), F32),
                 pltpu.VMEM((tile, tile), F32),
@@ -651,8 +684,8 @@
                 pltpu.VMEM((count, 2, 128), F32),
                 dma((6,)),
                 dma((6,)),
-                dma((4,)),
-                dma((4,)),
+                dma((5,)),
+                dma((5,)),
                 dma((count,)),
                 dma((count,)),
                 pltpu.SemaphoreType.REGULAR((4,)),

time: 26.9 us -> 26.1 us (0.970)
  Pallas kernels: 26.1 us -> 25.2 us
    pallas_call x1, Pallas kernels: 24.7 us -> 23.9 us  [shards(): pl.pallas_call(functools.partial(kernel, sizes), out_shape=(pltpu.VMEM(ti...]
where the time goes in v4:
time: 26.1 us; the launch traced here: 25.9 us
  Pallas kernels  25.2 us (97%)
  between operations  0.64 us (2%)
    pallas_call x1, Pallas kernels, shards(): pl.pallas_call(functools.partial(kernel, sizes), out_shape=(pltpu.VMEM(ti...  23.9 us
    pallas_call x1, Pallas kernels, shards(): pl.pallas_call(functools.partial(write, 1.0 / (site_count * sizes[0] * si...  1.35 us

profile of v4, /device:TPU:0, one launch (start us, length us, event | category | flops | bytes accessed | tf_op | source)
XLA Modules:
  0.0 25.9 jit_solution(17141240076384569502)
XLA Ops:
  0.6 23.9 %shard_map.218 = (f32[256,256]{1,0:T(8,128)S(1)}, f32[256,256]{1,0:T(8,128)S(1)}, f32[1,1,2,2048]{3,2,1,0:T(2,128)S(1)}, f32[8,128]{1,0:T(8,128)S(1)}) custom-call(f32[256,256]{1,0:T(8,128)} %refs_0_.1, s32[1,1,512]{2,1,0:T(1,128)} %refs_1_.1, s32[1,1,512]{2,1,0:T(1,128)} %refs_2_.1, s32[1,1,512]{2,1,0:T(1,128)} %refs_3_.1, s32[1,1,512]{2,1,0:T(1,128)} %refs_4_.1, ...), custom_call_target="tpu_custom_call" | custom-call | tf_op jit(solution)/shard_map/pallas_call | solution.py:659
  24.5 1.3 %shard_map.219 = (f32[256,256]{1,0:T(8,128)}, f32[256,256]{1,0:T(8,128)}, f32[1,1,2,2048]{3,2,1,0:T(2,128)}, f32[2]{0:T(128)}, f32[2]{0:T(128)}) custom-call(f32[256,256]{1,0:T(8,128)S(1)} %get-tuple-element.9.image, f32[256,256]{1,0:T(8,128)S(1)} %get-tuple-element.10.mask, f32[1,1,2,2048]{3,2,1,0:T(2,128)S(1)} %get-tuple-element.11.errors, ...), custom_call_target="tpu_custom_call" | custom-call | tf_op jit(solution)/shard_map/pallas_call | solution.py:700

commit v5 on v4

--- a/solution.py
+++ b/solution.py
@@ -540,8 +540,6 @@
     stat[1:2, :] = functools.reduce(
         jnp.add, [total[:, i : i + 128] for i in range(0, CHUNK, 128)]
     )
-    to_err = remote(err, err_rx, ka_send.at[3], ka_recv.at[3], partner)
-    to_err.start()
 
     def to_stat(offset):
         return remote(
@@ -552,11 +550,10 @@
             place(lax.rem(me + offset, count)),
         )
 
-    def send_stat(offset, carry):
+    for offset in sorted(range(1, count), key=lambda number: min(number, count - number)):
         to_stat(offset).start()
-        return carry
-
-    lax.fori_loop(1, count, send_stat, 0)
+    to_err = remote(err, err_rx, ka_send.at[3], ka_recv.at[3], partner)
+    to_err.start()
     stat_rx[pl.ds(me, 1)] = stat[...][None]
 
     to_img = remote(img, img_rx, ka_send.at[2], ka_recv.at[2], partner)

time: 26.1 us -> 26 us (level)
  no operation moved by 1% of the time
where the time goes in v5:
time: 26 us; the launch traced here: 25.8 us
  Pallas kernels  25.2 us (97%)
  between operations  0.64 us (2%)
    pallas_call x1, Pallas kernels, shards(): pl.pallas_call(functools.partial(kernel, sizes), out_shape=(pltpu.VMEM(ti...  23.9 us
    pallas_call x1, Pallas kernels, shards(): pl.pallas_call(functools.partial(write, 1.0 / (site_count * sizes[0] * si...  1.35 us

profile of v5, /device:TPU:0, one launch (start us, length us, event | category | flops | bytes accessed | tf_op | source)
XLA Modules:
  0.0 25.8 jit_solution(9962310261239958646)
XLA Ops:
  0.6 23.9 %shard_map.218 = (f32[256,256]{1,0:T(8,128)S(1)}, f32[256,256]{1,0:T(8,128)S(1)}, f32[1,1,2,2048]{3,2,1,0:T(2,128)S(1)}, f32[8,128]{1,0:T(8,128)S(1)}) custom-call(f32[256,256]{1,0:T(8,128)} %refs_0_.1, s32[1,1,512]{2,1,0:T(1,128)} %refs_1_.1, s32[1,1,512]{2,1,0:T(1,128)} %refs_2_.1, s32[1,1,512]{2,1,0:T(1,128)} %refs_3_.1, s32[1,1,512]{2,1,0:T(1,128)} %refs_4_.1, ...), custom_call_target="tpu_custom_call" | custom-call | tf_op jit(solution)/shard_map/pallas_call | solution.py:656
  24.5 1.3 %shard_map.219 = (f32[256,256]{1,0:T(8,128)}, f32[256,256]{1,0:T(8,128)}, f32[1,1,2,2048]{3,2,1,0:T(2,128)}, f32[2]{0:T(128)}, f32[2]{0:T(128)}) custom-call(f32[256,256]{1,0:T(8,128)S(1)} %get-tuple-element.9.image, f32[256,256]{1,0:T(8,128)S(1)} %get-tuple-element.10.mask, f32[1,1,2,2048]{3,2,1,0:T(2,128)S(1)} %get-tuple-element.11.errors, ...), custom_call_target="tpu_custom_call" | custom-call | tf_op jit(solution)/shard_map/pallas_call | solution.py:697
